TPU v7x, 32 devices: a whole 2x2x4 slice. The times are simulated.
32 devices in a mesh: groups: 2 (over y), ffn: 4 (over z), hidden: 4 (over x, core).
Axes of the slice: x: 2, y: 2, z: 4, core: 2. Of those that a mesh axis runs over, the one named last changes fastest.
Arguments:
- residual_in: bfloat16 [512, 8192], P(('groups', 'ffn'), 'hidden'), parts along dimension 0, may hold values from -10 to 10
- queries: bfloat16 [512, 8192], P(('groups', 'hidden'), 'ffn'), parts along dimension 0, may hold values from -100 to 100
- new_keys: bfloat16 [512, 1024], P(('groups', 'hidden'), 'ffn'), parts along dimension 0, may hold values from -6 to 6
- new_values: bfloat16 [512, 1024], P(('groups', 'hidden'), 'ffn'), parts along dimension 0, may hold values from -24 to 24
- key_cache: bfloat16 [32, 2048, 1024], P(('groups', 'hidden'), 'ffn'), parts along dimension 0, may hold values from -6 to 6
- value_cache: bfloat16 [32, 2048, 1024], P(('groups', 'hidden'), 'ffn'), parts along dimension 0, may hold values from -24 to 24
- cache_lengths: int32 [32], P(('groups', 'hidden')), parts along dimension 0, may hold values from 1 to 2048, as said below
- norm_gain: bfloat16 [8192], P('hidden'), may hold values from 0.099609375 to 1.8984375
- out_weight: bfloat16 [8192, 8192], P('ffn', 'hidden'), may hold values from -0.25 to 0.25
- gate_weight: bfloat16 [8192, 14336], P('hidden', 'ffn'), may hold values from -0.125 to 0.125
- up_weight: bfloat16 [8192, 14336], P('hidden', 'ffn'), may hold values from -0.125 to 0.125
- down_weight: bfloat16 [14336, 8192], P('ffn', 'hidden'), may hold values from -0.09375 to 0.09375
Outputs:
- block_out: bfloat16 [512, 8192], P(('groups', 'ffn'), 'hidden'), parts along dimension 0
There are 2 independent parts, one for each index of `groups`. A program takes and returns all parts, laid end to end along the dimension named above; an argument that names none is the same for every part. Nothing has to cross between parts.
Inputs may be any that keep to these rules, and one draw needn't show every extreme that they name: `cache_lengths`: each sequence's cached tokens fill the first cache positions; some sequence has exactly 2048.
All inputs are finite; a program needn't handle non-finite values.
Results may differ from a plain program's by a relative error of at most 0.04.
Values may be sent and summed in bfloat16 or wider, within the bound.
No kernel may reach another device: no remote copies, remote signals or barrier semaphores. Data moves between devices by JAX's collectives and lax.ppermute only.
A program may use at most 128 MiB of HBM per device.

v0:
```python
import math
import jax
import jax.numpy as jnp
from jax import lax
from jax.sharding import PartitionSpec as P

D = 8192
HEADS = 64
KVH = 8
HD = 128
DRAFT = 16


def rope_tables(positions, head_size):
    steps_half = jnp.arange(head_size // 2).astype(jnp.float32)
    inverse = jnp.exp(steps_half * (-2.0 * math.log(500000.0) / head_size))
    angle = positions.astype(jnp.float32)[:, None] * inverse[None, :]
    return (jnp.cos(angle), jnp.sin(angle))


def rotate(values, cosine, sine_table):
    half = values.shape[-1] // 2
    first_half = values[..., :half]
    second_half = values[..., half:]
    cosine = cosine[:, None, :]
    sine_table = sine_table[:, None, :]
    return jnp.concatenate(
        [
            first_half * cosine - second_half * sine_table,
            second_half * cosine + first_half * sine_table,
        ],
        axis=-1,
    )


def shards(
    residual_in,
    queries,
    new_keys,
    new_values,
    key_cache,
    value_cache,
    cache_lengths,
    norm_gain,
    out_weight,
    gate_weight,
    up_weight,
    down_weight,
):
    group = HEADS // KVH
    seq_count = cache_lengths.shape[0]
    block = key_cache.shape[1]
    query_all, key_fresh, value_fresh = (
        lax.all_gather(queries, "ffn", axis=1, tiled=True),
        lax.all_gather(new_keys, "ffn", axis=1, tiled=True),
        lax.all_gather(new_values, "ffn", axis=1, tiled=True),
    )
    positions = (cache_lengths[:, None] + jnp.arange(DRAFT, dtype=jnp.int32)[None, :]).reshape(-1)
    cosine, sine_table = rope_tables(positions, HD)
    query_rot = rotate(
        query_all.astype(jnp.float32).reshape(-1, HEADS, HD), cosine, sine_table
    ).astype(jnp.bfloat16)
    query_rot = query_rot.reshape(seq_count, DRAFT, KVH, group, HD)
    key_rot = rotate(key_fresh.astype(jnp.float32).reshape(-1, KVH, HD), cosine, sine_table).astype(
        jnp.bfloat16
    )
    key_rot = key_rot.reshape(seq_count, DRAFT, KVH, HD)
    value_rows = value_fresh.reshape(seq_count, DRAFT, KVH, HD)
    cached_keys = key_cache.reshape(seq_count, block, KVH, HD)
    cached_values = value_cache.reshape(seq_count, block, KVH, HD)
    scaling = 1.0 / math.sqrt(HD)
    cache_scores = (
        jnp.einsum("sjkgd,spkd->sjkgp", query_rot, cached_keys, preferred_element_type=jnp.float32)
        * scaling
    )
    draft_scores = (
        jnp.einsum("sjkgd,sikd->sjkgi", query_rot, key_rot, preferred_element_type=jnp.float32)
        * scaling
    )
    ffn_index = lax.axis_index("ffn")
    slot_positions = ffn_index * block + jnp.arange(block, dtype=jnp.int32)
    usable = (slot_positions[None, :] < cache_lengths[:, None])[:, None, None, None, :]
    causal = jnp.arange(DRAFT)[None, :] <= jnp.arange(DRAFT)[:, None]
    draft_usable = jnp.logical_and(causal[None, :, None, None, :], ffn_index == 0)
    cache_scores = jnp.where(usable, cache_scores, -1e30)
    draft_scores = jnp.where(draft_usable, draft_scores, -1e30)
    local_peak = jnp.maximum(cache_scores.max(-1), draft_scores.max(-1))
    peak_score = lax.pmax(local_peak, "ffn")[..., None]
    cache_weights = jnp.where(usable, jnp.exp(cache_scores - peak_score), 0.0)
    draft_weights = jnp.where(draft_usable, jnp.exp(draft_scores - peak_score), 0.0)
    numerator = jnp.einsum(
        "sjkgp,spkd->sjkgd",
        cache_weights.astype(jnp.bfloat16),
        cached_values,
        preferred_element_type=jnp.float32,
    )
    numerator = numerator + jnp.einsum(
        "sjkgi,sikd->sjkgd",
        draft_weights.astype(jnp.bfloat16),
        value_rows,
        preferred_element_type=jnp.float32,
    )
    denominator = cache_weights.sum(-1) + draft_weights.sum(-1)
    row_count = seq_count * DRAFT
    numerator = numerator.reshape(row_count, HEADS, HD)
    denominator = denominator.reshape(row_count, HEADS)
    heads_here = out_weight.shape[0] // HD
    numerator_share, denominator_share = (
        lax.psum_scatter(
            numerator.astype(jnp.bfloat16), "ffn", scatter_dimension=1, tiled=True
        ).astype(jnp.float32),
        lax.psum_scatter(
            denominator.astype(jnp.bfloat16), "ffn", scatter_dimension=1, tiled=True
        ).astype(jnp.float32),
    )
    attended = (
        (numerator_share / denominator_share[..., None])
        .reshape(row_count, heads_here * HD)
        .astype(jnp.bfloat16)
    )
    attended_rows = lax.all_gather(attended, "hidden", axis=0, tiled=True)
    projected = lax.psum_scatter(
        jnp.dot(attended_rows, out_weight, preferred_element_type=jnp.float32).astype(jnp.bfloat16),
        "ffn",
        scatter_dimension=0,
        tiled=True,
    ).astype(jnp.float32)
    resid = (residual_in.astype(jnp.float32) + projected).astype(jnp.bfloat16)
    widened = resid.astype(jnp.float32)
    squares = lax.psum(jnp.sum(widened * widened, axis=1), "hidden")
    factor = lax.rsqrt(squares / D + 1e-05)[:, None]
    normed = (widened * factor * norm_gain.astype(jnp.float32)[None, :]).astype(jnp.bfloat16)
    units_here = gate_weight.shape[1]
    piece = lax.all_gather(normed, "ffn", axis=0, tiled=True)
    partial_inner = jnp.concatenate(
        [
            jnp.dot(piece, gate_weight, preferred_element_type=jnp.float32),
            jnp.dot(piece, up_weight, preferred_element_type=jnp.float32),
        ],
        axis=1,
    )
    summed = lax.psum(partial_inner.astype(jnp.bfloat16), "hidden").astype(jnp.float32)
    activation = (jax.nn.silu(summed[:, :units_here]) * summed[:, units_here:]).astype(jnp.bfloat16)
    lowered = lax.psum_scatter(
        jnp.dot(activation, down_weight, preferred_element_type=jnp.float32).astype(jnp.bfloat16),
        "ffn",
        scatter_dimension=0,
        tiled=True,
    ).astype(jnp.float32)
    return (widened + lowered).astype(jnp.bfloat16)


def solution(mesh):
    in_specs = (
        P(("groups", "ffn"), "hidden"),
        P(("groups", "hidden"), "ffn"),
        P(("groups", "hidden"), "ffn"),
        P(("groups", "hidden"), "ffn"),
        P(("groups", "hidden"), "ffn", None),
        P(("groups", "hidden"), "ffn", None),
        P(("groups", "hidden")),
        P("hidden"),
        P("ffn", "hidden"),
        P("hidden", "ffn"),
        P("hidden", "ffn"),
        P("ffn", "hidden"),
    )
    out_specs = P(("groups", "ffn"), "hidden")
    return jax.shard_map(shards, mesh=mesh, in_specs=in_specs, out_specs=out_specs, check_vma=False)
```

profile of v0, /device:TPU:0, one launch (start us, length us, event | category | flops | bytes accessed | tf_op | source)
XLA Modules:
  0.0 375.5 jit_solution(9837612590256703097)
XLA Ops:
  8.1 15.4 %all_gather.16 = bf16[64,1024]{1,0:T(8,128)(2,1)S(1)} all-gather(bf16[64,256]{1,0:T(8,128)(2,1)} %param.14), channel_id=1, replica_groups=mesh['groups'=2,'ffn'=4,'hidden'=4] {'ffn'}, dimensions={1}, use_global_device_ids=true | all-gather | bytes 163840 | tf_op jit(solution)/shard_map/all_gather | solution.py:55
  24.0 15.5 %all_gather.17 = bf16[64,1024]{1,0:T(8,128)(2,1)S(1)} all-gather(bf16[64,256]{1,0:T(8,128)(2,1)} %param.15), channel_id=1, replica_groups=mesh['groups'=2,'ffn'=4,'hidden'=4] {'ffn'}, dimensions={1}, use_global_device_ids=true | all-gather | bytes 163840 | tf_op jit(solution)/shard_map/all_gather | solution.py:56
  39.5 3.5 copy.87
  44.9 2.2 bitcast_bitcast_fusion.1
  47.1 2.2 bitcast_bitcast_fusion
  52.6 2.6 fusion.16
  55.4 7.1 %bitcast_reduce_fusion = (f32[4,16,8,8]{3,1,2,0:T(8,128)S(1)}, f32[4,8,16,8,512]{4,3,2,1,0:T(8,128)}) fusion(pred[4,512]{1,0:T(4,128)(4,1)S(1)} %broadcast_compare_fusion, bf16[4,512,8,128,1]{3,2,1,0,4:T(8,128)(2,1)} %bitcast_bitcast_fusion.1, bf16[4,16,8,8,128]{4,3,2,1,0:T(8,128)(2,1)S(1)} %pad_maximum_fusion.1), kind=kOutput, calls=%fused_computation.1 | convolution fusion | flops 543158272 | bytes 13649920 | tf_op jit(solution)/shard_map/sjkgd,spkd->sjkgp/dot_general | solution.py:73
  62.5 24.8 %pmax.7 = f32[4,16,8,8]{3,1,2,0:T(8,128)S(1)} all-reduce(f32[4,16,8,8]{3,1,2,0:T(8,128)S(1)} %max.5), channel_id=1, replica_groups=mesh['groups'=2,'ffn'=4,'hidden'=4] {'ffn'}, use_global_device_ids=true, to_apply=%region_2.3 | all-reduce | flops 4096 | bytes 32768 | tf_op jit(solution)/shard_map/pmax | solution.py:88
  87.5 4.7 %fusion.2 = f32[4,16,8,8]{3,1,2,0:T(8,128)S(1)} fusion(f32[4,8,16,8,512]{4,3,2,1,0:T(8,128)} %get-tuple-element.14, f32[4,16,8,8]{3,1,2,0:T(8,128)S(1)} %pmax.7, pred[4,512]{1,0:T(4,128)(4,1)S(1)} %broadcast_compare_fusion), kind=kLoop, calls=%fused_computation.5 | loop fusion | flops 10481664 | bytes 8423424 | tf_op jit(solution)/shard_map/reduce_sum | solution.py:103
  96.5 7.0 %fusion.4 = f32[4,8,16,8,128]{4,3,2,1,0:T(8,128)S(1)} fusion(f32[4,8,16,8,512]{4,3,2,1,0:T(8,128)} %get-tuple-element.14, bf16[4,512,8,128,1]{3,2,1,0,4:T(8,128)(2,1)} %bitcast_bitcast_fusion, f32[4,16,8,8]{3,1,2,0:T(8,128)S(1)} %pmax.7, pred[4,512]{1,0:T(4,128)(4,1)S(1)} %broadcast_compare_fusion), kind=kOutput, calls=%fused_computation.9 | convolution fusion | flops 547356672 | bytes 14698496 | tf_op jit(solution)/shard_map/sjkgp,spkd->sjkgd/dot_general | solution.py:91
  105.3 8.2 %reduce-scatter.7.cloned.1.call-done = bf16[64,16]{0,1:T(8,128)(2,1)} async-done(((bf16[64,64]{0,1:T(8,128)(2,1)}), bf16[64,16]{0,1:T(8,128)(2,1)}) %reduce-scatter.7.cloned.1.call-update) | async-done | bytes 2064 | tf_op jit(solution)/shard_map/reduce_scatter | solution.py:112
  114.3 27.0 %reduce-scatter.5.cloned.1.call-done = bf16[64,16,128]{2,1,0:T(8,128)(2,1)} async-done(((bf16[64,64,128]{2,1,0:T(8,128)(2,1)}), bf16[64,16,128]{2,1,0:T(8,128)(2,1)}) %reduce-scatter.5.cloned.1.call-update) | async-done | bytes 262160 | tf_op jit(solution)/shard_map/reduce_scatter | solution.py:109
  143.3 15.3 %all-gather.6.cloned.1.call-done = bf16[256,2048]{1,0:T(8,128)(2,1)} async-done(((bf16[64,2048]{1,0:T(8,128)(2,1)}), bf16[256,2048]{1,0:T(8,128)(2,1)}) %all-gather.6.cloned.1.call-update) | async-done | bytes 1048592 | tf_op jit(solution)/shard_map/all_gather | solution.py:121
  158.6 7.0 %convolution_convert_fusion.3 = bf16[256,2048]{1,0:T(8,128)(2,1)} fusion(bf16[256,2048]{1,0:T(8,128)(2,1)} %all-gather.6.cloned.1.call-done, bf16[2048,2048]{1,0:T(8,128)(2,1)} %param.20), kind=kOutput, calls=%fused_computation.25 | convolution fusion | flops 2148007936 | bytes 10485760 | tf_op jit(solution)/shard_map/dot_general | solution.py:123
  165.7 27.4 %reduce-scatter.9.cloned.1.call-done = bf16[64,2048]{1,0:T(8,128)(2,1)} async-done(((bf16[256,2048]{1,0:T(8,128)(2,1)}), bf16[64,2048]{1,0:T(8,128)(2,1)}) %reduce-scatter.9.cloned.1.call-update) | async-done | bytes 262160 | tf_op jit(solution)/shard_map/reduce_scatter | solution.py:122
  194.2 6.2 %psum.14 = f32[64]{0:T(128)S(1)} all-reduce(f32[64]{0:T(128)S(1)} %fusion.25), channel_id=1, replica_groups=mesh['groups'=2,'ffn'=4,'hidden'=4] {'hidden'}, use_global_device_ids=true, to_apply=%region_9.10 | all-reduce | flops 64 | bytes 512 | tf_op jit(solution)/shard_map/psum | solution.py:130
  202.5 26.1 %all-gather.8.cloned.1.call-done = bf16[256,2048]{1,0:T(8,128)(2,1)} async-done(((bf16[64,2048]{1,0:T(8,128)(2,1)}), bf16[256,2048]{1,0:T(8,128)(2,1)}) %all-gather.8.cloned.1.call-update) | async-done | bytes 1048592 | tf_op jit(solution)/shard_map/all_gather | solution.py:134
  228.6 9.5 %convolution_convert_fusion = bf16[256,3584]{1,0:T(8,128)(2,1)S(1)} fusion(bf16[256,2048]{1,0:T(8,128)(2,1)} %all-gather.8.cloned.1.call-done, bf16[2048,3584]{1,0:T(8,128)(2,1)} %param.22), kind=kOutput, calls=%fused_computation.7 | convolution fusion | flops 3759013888 | bytes 17563648 | tf_op jit(solution)/shard_map/dot_general | solution.py:138
  238.2 9.1 %convolution_convert_fusion.1 = bf16[256,3584]{1,0:T(8,128)(2,1)S(1)} fusion(bf16[256,2048]{1,0:T(8,128)(2,1)S(1)} %copy-done.6, bf16[2048,3584]{1,0:T(8,128)(2,1)} %param.21), kind=kOutput, calls=%fused_computation.8 | convolution fusion | flops 3759013888 | bytes 17563648 | tf_op jit(solution)/shard_map/dot_general | solution.py:137
  247.3 2.3 pad_maximum_fusion
  249.6 76.5 %all-reduce.2.cloned.1.call-done = bf16[256,7168]{1,0:T(8,128)(2,1)} async-done(((bf16[256,7168]{1,0:T(8,128)(2,1)}), bf16[256,7168]{1,0:T(8,128)(2,1)}) %all-reduce.2.cloned.1.call-update) | async-done | bytes 3670032 | tf_op jit(solution)/shard_map/psum | solution.py:142
  326.1 2.9 convert_element_type.114
  329.0 10.3 %convolution_convert_fusion.2 = bf16[256,2048]{1,0:T(8,128)(2,1)} fusion(bf16[3584,2048]{1,0:T(8,128)(2,1)} %param.23, f32[256,7168]{1,0:T(8,128)S(1)} %convert_element_type.114), kind=kOutput, calls=%fused_computation.24 | convolution fusion | flops 3764125696 | bytes 23068672 | tf_op jit(solution)/shard_map/dot_general | solution.py:145
  339.3 27.6 %reduce-scatter.11.cloned.1.call-done = bf16[64,2048]{1,0:T(8,128)(2,1)} async-done(((bf16[256,2048]{1,0:T(8,128)(2,1)}), bf16[64,2048]{1,0:T(8,128)(2,1)}) %reduce-scatter.11.cloned.1.call-update) | async-done | bytes 262160 | tf_op jit(solution)/shard_map/reduce_scatter | solution.py:144
  (69 shorter events, 21.3 us)
Async XLA Ops:
  6.5 42.8 %all-gather.4.cloned.1.call-start = ((), (), s32[]{:S(2)}) async-start(), calls=%async_computation.4 | async-start | bytes 1310720 | tf_op jit(solution)/shard_map/all_gather | solution.py:54
  7.3 106.3 %reduce-scatter.7.cloned.1.call-start = ((), (), s32[]{:S(2)}) async-start(), calls=%async_computation.6 | async-start | bytes 20480 | tf_op jit(solution)/shard_map/reduce_scatter | solution.py:112
  39.5 3.5 copy-start
  43.0 1.2 copy-start.5
  95.6 45.7 %reduce-scatter.5.cloned.1.call-start = ((), (), s32[]{:S(2)}) async-start(), calls=%async_computation.5 | async-start | bytes 1310720 | tf_op jit(solution)/shard_map/reduce_scatter | solution.py:109
  96.5 7.0 %copy-start.3 = (bf16[4,16,8,128,1]{3,2,1,0,4:T(8,128)(2,1)S(1)}, bf16[4,16,8,128,1]{3,2,1,0,4:T(8,128)(2,1)}, u32[]{:S(2)}) copy-start(bf16[4,16,8,128,1]{3,2,1,0,4:T(8,128)(2,1)} %bitcast_bitcast_fusion.2) | copy-start | bytes 393220
  105.2 53.4 %all-gather.6.cloned.1.call-start = ((), (), s32[]{:S(2)}) async-start(), calls=%async_computation.7 | async-start | bytes 1310720 | tf_op jit(solution)/shard_map/all_gather | solution.py:121
  143.3 22.4 %copy-start.4 = (bf16[2048]{0:T(1024)(128)(2,1)S(1)}, bf16[2048]{0:T(1024)(128)(2,1)}, u32[]{:S(2)}) copy-start(bf16[2048]{0:T(1024)(128)(2,1)} %param.19) | copy-start | bytes 12292
  143.3 49.8 %copy-start.1 = (bf16[64,2048]{1,0:T(8,128)(2,1)S(1)}, bf16[64,2048]{1,0:T(8,128)(2,1)}, u32[]{:S(2)}) copy-start(bf16[64,2048]{1,0:T(8,128)(2,1)} %param.12) | copy-start | bytes 786436
  143.3 49.8 %reduce-scatter.9.cloned.1.call-start = ((), (), s32[]{:S(2)}) async-start(), calls=%async_computation.8 | async-start | bytes 1310720 | tf_op jit(solution)/shard_map/reduce_scatter | solution.py:122
  165.7 63.0 %all-gather.8.cloned.1.call-start = ((), (), s32[]{:S(2)}) async-start(), calls=%async_computation.9 | async-start | bytes 1310720 | tf_op jit(solution)/shard_map/all_gather | solution.py:134
  202.2 123.9 %all-reduce.2.cloned.1.call-start = ((), (), s32[]{:S(2)}) async-start(), calls=%async_computation.10 | async-start | bytes 7340032 | tf_op jit(solution)/shard_map/psum | solution.py:142
  228.6 9.5 %copy-start.6 = (bf16[256,2048]{1,0:T(8,128)(2,1)S(1)}, bf16[256,2048]{1,0:T(8,128)(2,1)}, u32[]{:S(2)}) copy-start(bf16[256,2048]{1,0:T(8,128)(2,1)} %all-gather.8.cloned.1.call-done) | copy-start | bytes 3145732
  249.6 117.3 %reduce-scatter.11.cloned.1.call-start = ((), (), s32[]{:S(2)}) async-start(), calls=%async_computation.11 | async-start | bytes 1310720 | tf_op jit(solution)/shard_map/reduce_scatter | solution.py:144
  329.0 37.9 %copy-start.2 = (bf16[64,2048]{1,0:T(8,128)(2,1)S(1)}, bf16[64,2048]{1,0:T(8,128)(2,1)}, u32[]{:S(2)}) copy-start(bf16[64,2048]{1,0:T(8,128)(2,1)} %reduce-scatter.9.cloned.1.call-done) | copy-start | bytes 786436
Sparse Core Ops, SparseCore 0:
  8.9 33.5 all-gather.3
  95.8 17.7 reduce-scatter.6
  115.8 25.4 reduce-scatter.4
  143.4 15.1 all-gather.5
  165.8 27.2 reduce-scatter.8
  202.3 26.2 all-gather.7
  249.7 76.3 all-reduce.1
  339.4 27.4 reduce-scatter.10
where the time goes:
time: 376 us; the launch traced here: 375 us
  waiting for transfers between devices  209 us (56%)
  blocking collectives  61.9 us (16%)
  matrix products  53.1 us (14%)
  other arithmetic  21.6 us (6%)
  local copies, waits for them, and re-layouts  15.6 us (4%)
  between operations  13.8 us (4%)
    psum x1, waiting for transfers between devices, shards(): lax.psum(partial_inner.astype(jnp.bfloat16), 'hidden').astype(jnp.float32)  76.5 us
    reduce_scatter x1, waiting for transfers between devices, shards(): lax.psum_scatter(jnp.dot(activation, down_weight, preferred_element_type=...  27.6 us
    reduce_scatter x1, waiting for transfers between devices, shards(): lax.psum_scatter(jnp.dot(attended_rows, out_weight, preferred_element_typ...  27.4 us
    reduce_scatter x1, waiting for transfers between devices, shards(): lax.psum_scatter(numerator.astype(jnp.bfloat16), 'ffn', scatter_dimension...  27 us
    all_gather x1, waiting for transfers between devices, shards(): piece = lax.all_gather(normed, 'ffn', axis=0, tiled=True)  26.1 us
    pmax x1, blocking collectives, shards(): peak_score = lax.pmax(local_peak, 'ffn')[..., None]  24.8 us
    all_gather x1, blocking collectives, shards(): lax.all_gather(new_values, 'ffn', axis=1, tiled=True)  15.5 us
    all_gather x1, blocking collectives, shards(): lax.all_gather(new_keys, 'ffn', axis=1, tiled=True)  15.4 us
  transfers between devices with their start and end apart: 8, of which 7 were waited for; matrix products, arithmetic and copies ran while one was open for 6% of the time, Pallas kernels for 0%

commit v1 on v0

--- a/solution.py
+++ b/solution.py
@@ -139,7 +139,9 @@
         ],
         axis=1,
     )
-    summed = lax.psum(partial_inner.astype(jnp.bfloat16), "hidden").astype(jnp.float32)
+    summed = jnp.sum(lax.all_gather(partial_inner.astype(jnp.bfloat16), "hidden"), axis=0).astype(
+        jnp.float32
+    )
     activation = (jax.nn.silu(summed[:, :units_here]) * summed[:, units_here:]).astype(jnp.bfloat16)
     lowered = lax.psum_scatter(
         jnp.dot(activation, down_weight, preferred_element_type=jnp.float32).astype(jnp.bfloat16),

time: 376 us -> 404 us (1.074)
  waiting for transfers between devices: 209 us -> 226 us
  other arithmetic: 21.6 us -> 32.5 us
    all_gather x0 -> x1, waiting for transfers between devices: none -> 93.5 us  [shards(): lax.all_gather(partial_inner.astype(jnp.bfloat16), 'hidden')]
    psum x1 -> x0, waiting for transfers between devices: 76.5 us -> none  [shards(): lax.psum(partial_inner.astype(jnp.bfloat16), 'hidden').astype(jnp.float32)]
    reduce_sum x0 -> x1, other arithmetic: none -> 10.9 us  [shards(): jnp.sum(lax.all_gather(partial_inner.astype(jnp.bfloat16), 'hidden'), axi...]
  transfers between devices with their start and end apart: 8 -> 8, of which waited for: 7 -> 7; matrix products, arithmetic and copies ran while one was open for 6% -> 5% of each run, Pallas kernels for 0% -> 0%
where the time goes in v1:
time: 404 us; the launch traced here: 403 us
  waiting for transfers between devices  226 us (56%)
  blocking collectives  61.9 us (15%)
  matrix products  53.1 us (13%)
  other arithmetic  32.5 us (8%)
  local copies, waits for them, and re-layouts  15.6 us (4%)
  between operations  13.8 us (3%)
    all_gather x1, waiting for transfers between devices, shards(): lax.all_gather(partial_inner.astype(jnp.bfloat16), 'hidden')  93.5 us
    reduce_scatter x1, waiting for transfers between devices, shards(): lax.psum_scatter(jnp.dot(activation, down_weight, preferred_element_type=...  27.4 us
    reduce_scatter x1, waiting for transfers between devices, shards(): lax.psum_scatter(jnp.dot(attended_rows, out_weight, preferred_element_typ...  27.4 us
    reduce_scatter x1, waiting for transfers between devices, shards(): lax.psum_scatter(numerator.astype(jnp.bfloat16), 'ffn', scatter_dimension...  27 us
    all_gather x1, waiting for transfers between devices, shards(): piece = lax.all_gather(normed, 'ffn', axis=0, tiled=True)  26.1 us
    pmax x1, blocking collectives, shards(): peak_score = lax.pmax(local_peak, 'ffn')[..., None]  24.8 us
    all_gather x1, blocking collectives, shards(): lax.all_gather(new_values, 'ffn', axis=1, tiled=True)  15.5 us
    all_gather x1, blocking collectives, shards(): lax.all_gather(new_keys, 'ffn', axis=1, tiled=True)  15.4 us
  transfers between devices with their start and end apart: 8, of which 7 were waited for; matrix products, arithmetic and copies ran while one was open for 5% of the time, Pallas kernels for 0%

profile of v1, /device:TPU:0, one launch (start us, length us, event | category | flops | bytes accessed | tf_op | source)
XLA Modules:
  0.0 403.2 jit_solution(10199359274937772993)
XLA Ops:
  8.1 15.4 %all_gather.20 = bf16[64,1024]{1,0:T(8,128)(2,1)S(1)} all-gather(bf16[64,256]{1,0:T(8,128)(2,1)} %param.14), channel_id=1, replica_groups=mesh['groups'=2,'ffn'=4,'hidden'=4] {'ffn'}, dimensions={1}, use_global_device_ids=true | all-gather | bytes 163840 | tf_op jit(solution)/shard_map/all_gather | solution.py:55
  24.0 15.5 %all_gather.21 = bf16[64,1024]{1,0:T(8,128)(2,1)S(1)} all-gather(bf16[64,256]{1,0:T(8,128)(2,1)} %param.15), channel_id=1, replica_groups=mesh['groups'=2,'ffn'=4,'hidden'=4] {'ffn'}, dimensions={1}, use_global_device_ids=true | all-gather | bytes 163840 | tf_op jit(solution)/shard_map/all_gather | solution.py:56
  39.6 3.5 copy.87
  44.9 2.2 bitcast_bitcast_fusion.1
  47.1 2.2 bitcast_bitcast_fusion
  52.6 2.6 fusion.18
  55.4 7.1 %bitcast_reduce_fusion = (f32[4,16,8,8]{3,1,2,0:T(8,128)S(1)}, f32[4,8,16,8,512]{4,3,2,1,0:T(8,128)}) fusion(pred[4,512]{1,0:T(4,128)(4,1)S(1)} %broadcast_compare_fusion, bf16[4,512,8,128,1]{3,2,1,0,4:T(8,128)(2,1)} %bitcast_bitcast_fusion.1, bf16[4,16,8,8,128]{4,3,2,1,0:T(8,128)(2,1)S(1)} %pad_maximum_fusion.1), kind=kOutput, calls=%fused_computation.1 | convolution fusion | flops 543158272 | bytes 13649920 | tf_op jit(solution)/shard_map/sjkgd,spkd->sjkgp/dot_general | solution.py:73
  62.5 24.8 %pmax.7 = f32[4,16,8,8]{3,1,2,0:T(8,128)S(1)} all-reduce(f32[4,16,8,8]{3,1,2,0:T(8,128)S(1)} %max.5), channel_id=1, replica_groups=mesh['groups'=2,'ffn'=4,'hidden'=4] {'ffn'}, use_global_device_ids=true, to_apply=%region_2.3 | all-reduce | flops 4096 | bytes 32768 | tf_op jit(solution)/shard_map/pmax | solution.py:88
  87.5 4.7 %fusion.2 = f32[4,16,8,8]{3,1,2,0:T(8,128)S(1)} fusion(f32[4,8,16,8,512]{4,3,2,1,0:T(8,128)} %get-tuple-element.14, f32[4,16,8,8]{3,1,2,0:T(8,128)S(1)} %pmax.7, pred[4,512]{1,0:T(4,128)(4,1)S(1)} %broadcast_compare_fusion), kind=kLoop, calls=%fused_computation.5 | loop fusion | flops 10481664 | bytes 8423424 | tf_op jit(solution)/shard_map/reduce_sum | solution.py:103
  96.5 7.0 %fusion.6 = f32[4,8,16,8,128]{4,3,2,1,0:T(8,128)S(1)} fusion(f32[4,8,16,8,512]{4,3,2,1,0:T(8,128)} %get-tuple-element.14, bf16[4,512,8,128,1]{3,2,1,0,4:T(8,128)(2,1)} %bitcast_bitcast_fusion, f32[4,16,8,8]{3,1,2,0:T(8,128)S(1)} %pmax.7, pred[4,512]{1,0:T(4,128)(4,1)S(1)} %broadcast_compare_fusion), kind=kOutput, calls=%fused_computation.11 | convolution fusion | flops 547356672 | bytes 14698496 | tf_op jit(solution)/shard_map/sjkgp,spkd->sjkgd/dot_general | solution.py:91
  105.3 8.2 %reduce-scatter.7.cloned.1.call-done = bf16[64,16]{0,1:T(8,128)(2,1)} async-done(((bf16[64,64]{0,1:T(8,128)(2,1)}), bf16[64,16]{0,1:T(8,128)(2,1)}) %reduce-scatter.7.cloned.1.call-update) | async-done | bytes 2064 | tf_op jit(solution)/shard_map/reduce_scatter | solution.py:112
  114.3 27.0 %reduce-scatter.5.cloned.1.call-done = bf16[64,16,128]{2,1,0:T(8,128)(2,1)} async-done(((bf16[64,64,128]{2,1,0:T(8,128)(2,1)}), bf16[64,16,128]{2,1,0:T(8,128)(2,1)}) %reduce-scatter.5.cloned.1.call-update) | async-done | bytes 262160 | tf_op jit(solution)/shard_map/reduce_scatter | solution.py:109
  143.3 15.3 %all-gather.7.cloned.1.call-done = bf16[256,2048]{1,0:T(8,128)(2,1)} async-done(((bf16[64,2048]{1,0:T(8,128)(2,1)}), bf16[256,2048]{1,0:T(8,128)(2,1)}) %all-gather.7.cloned.1.call-update) | async-done | bytes 1048592 | tf_op jit(solution)/shard_map/all_gather | solution.py:121
  158.6 7.0 %convolution_convert_fusion.3 = bf16[256,2048]{1,0:T(8,128)(2,1)} fusion(bf16[256,2048]{1,0:T(8,128)(2,1)} %all-gather.7.cloned.1.call-done, bf16[2048,2048]{1,0:T(8,128)(2,1)} %param.20), kind=kOutput, calls=%fused_computation.27 | convolution fusion | flops 2148007936 | bytes 10485760 | tf_op jit(solution)/shard_map/dot_general | solution.py:123
  165.7 27.4 %reduce-scatter.9.cloned.1.call-done = bf16[64,2048]{1,0:T(8,128)(2,1)} async-done(((bf16[256,2048]{1,0:T(8,128)(2,1)}), bf16[64,2048]{1,0:T(8,128)(2,1)}) %reduce-scatter.9.cloned.1.call-update) | async-done | bytes 262160 | tf_op jit(solution)/shard_map/reduce_scatter | solution.py:122
  194.2 6.2 %psum.7 = f32[64]{0:T(128)S(1)} all-reduce(f32[64]{0:T(128)S(1)} %fusion.27), channel_id=1, replica_groups=mesh['groups'=2,'ffn'=4,'hidden'=4] {'hidden'}, use_global_device_ids=true, to_apply=%region_9.10 | all-reduce | flops 64 | bytes 512 | tf_op jit(solution)/shard_map/psum | solution.py:130
  202.5 26.1 %all-gather.9.cloned.1.call-done = bf16[256,2048]{1,0:T(8,128)(2,1)} async-done(((bf16[64,2048]{1,0:T(8,128)(2,1)}), bf16[256,2048]{1,0:T(8,128)(2,1)}) %all-gather.9.cloned.1.call-update) | async-done | bytes 1048592 | tf_op jit(solution)/shard_map/all_gather | solution.py:134
  228.6 9.5 %fusion.5 = bf16[1,256,3584]{2,1,0:T(8,128)(2,1)S(1)} fusion(bf16[256,2048]{1,0:T(8,128)(2,1)} %all-gather.9.cloned.1.call-done, bf16[2048,3584]{1,0:T(8,128)(2,1)} %param.22), kind=kOutput, calls=%fused_computation.10 | convolution fusion | flops 3759013888 | bytes 17563648 | tf_op jit(solution)/shard_map/dot_general | solution.py:138
  238.2 9.1 %fusion.4 = bf16[1,256,3584]{2,1,0:T(8,128)(2,1)S(1)} fusion(bf16[256,2048]{1,0:T(8,128)(2,1)S(1)} %copy-done.6, bf16[2048,3584]{1,0:T(8,128)(2,1)} %param.21), kind=kOutput, calls=%fused_computation.9 | convolution fusion | flops 3759013888 | bytes 17563648 | tf_op jit(solution)/shard_map/dot_general | solution.py:137
  249.6 93.5 %all-gather.11.cloned.1.call-done = bf16[4,256,7168]{2,1,0:T(8,128)(2,1)} async-done(((bf16[1,256,7168]{2,1,0:T(8,128)(2,1)}), bf16[4,256,7168]{2,1,0:T(8,128)(2,1)}) %all-gather.11.cloned.1.call-update) | async-done | bytes 14680080 | tf_op jit(solution)/shard_map/all_gather | solution.py:142
  343.0 10.9 %reduce_sum.42 = bf16[256,7168]{1,0:T(8,128)(2,1)} reduce(bf16[4,256,7168]{2,1,0:T(8,128)(2,1)} %all-gather.11.cloned.1.call-done, bf16[]{:T(256)} %constant.28.clone.1), dimensions={0}, to_apply=%region_10.11 | reduce | flops 5505024 | bytes 18350082 | tf_op jit(solution)/shard_map/reduce_sum | solution.py:142
  353.9 2.9 convert_element_type.123
  356.8 10.3 %convolution_convert_fusion.2 = bf16[256,2048]{1,0:T(8,128)(2,1)} fusion(bf16[3584,2048]{1,0:T(8,128)(2,1)} %param.23, f32[256,7168]{1,0:T(8,128)S(1)} %convert_element_type.123), kind=kOutput, calls=%fused_computation.26 | convolution fusion | flops 3764125696 | bytes 23068672 | tf_op jit(solution)/shard_map/dot_general | solution.py:147
  367.2 27.4 %reduce-scatter.11.cloned.1.call-done = bf16[64,2048]{1,0:T(8,128)(2,1)} async-done(((bf16[256,2048]{1,0:T(8,128)(2,1)}), bf16[64,2048]{1,0:T(8,128)(2,1)}) %reduce-scatter.11.cloned.1.call-update) | async-done | bytes 262160 | tf_op jit(solution)/shard_map/reduce_scatter | solution.py:146
  (70 shorter events, 23.5 us)
Async XLA Ops:
  6.5 42.8 %all-gather.5.cloned.1.call-start = ((), (), s32[]{:S(2)}) async-start(), calls=%async_computation.4 | async-start | bytes 1310720 | tf_op jit(solution)/shard_map/all_gather | solution.py:54
  7.3 106.3 %reduce-scatter.7.cloned.1.call-start = ((), (), s32[]{:S(2)}) async-start(), calls=%async_computation.6 | async-start | bytes 20480 | tf_op jit(solution)/shard_map/reduce_scatter | solution.py:112
  39.5 3.5 copy-start
  43.0 1.1 copy-start.5
  95.7 45.7 %reduce-scatter.5.cloned.1.call-start = ((), (), s32[]{:S(2)}) async-start(), calls=%async_computation.5 | async-start | bytes 1310720 | tf_op jit(solution)/shard_map/reduce_scatter | solution.py:109
  96.5 7.0 %copy-start.3 = (bf16[4,16,8,128,1]{3,2,1,0,4:T(8,128)(2,1)S(1)}, bf16[4,16,8,128,1]{3,2,1,0,4:T(8,128)(2,1)}, u32[]{:S(2)}) copy-start(bf16[4,16,8,128,1]{3,2,1,0,4:T(8,128)(2,1)} %bitcast_bitcast_fusion.2) | copy-start | bytes 393220
  105.2 53.4 %all-gather.7.cloned.1.call-start = ((), (), s32[]{:S(2)}) async-start(), calls=%async_computation.7 | async-start | bytes 1310720 | tf_op jit(solution)/shard_map/all_gather | solution.py:121
  143.3 22.4 %copy-start.4 = (bf16[2048]{0:T(1024)(128)(2,1)S(1)}, bf16[2048]{0:T(1024)(128)(2,1)}, u32[]{:S(2)}) copy-start(bf16[2048]{0:T(1024)(128)(2,1)} %param.19) | copy-start | bytes 12292
  143.3 49.8 %copy-start.1 = (bf16[64,2048]{1,0:T(8,128)(2,1)S(1)}, bf16[64,2048]{1,0:T(8,128)(2,1)}, u32[]{:S(2)}) copy-start(bf16[64,2048]{1,0:T(8,128)(2,1)} %param.12) | copy-start | bytes 786436
  143.3 49.8 %reduce-scatter.9.cloned.1.call-start = ((), (), s32[]{:S(2)}) async-start(), calls=%async_computation.8 | async-start | bytes 1310720 | tf_op jit(solution)/shard_map/reduce_scatter | solution.py:122
  165.7 63.0 %all-gather.9.cloned.1.call-start = ((), (), s32[]{:S(2)}) async-start(), calls=%async_computation.9 | async-start | bytes 1310720 | tf_op jit(solution)/shard_map/all_gather | solution.py:134
  202.2 140.8 %all-gather.11.cloned.1.call-start = ((), (), s32[]{:S(2)}) async-start(), calls=%async_computation.10 | async-start | bytes 18350080 | tf_op jit(solution)/shard_map/all_gather | solution.py:142
  228.6 9.5 %copy-start.6 = (bf16[256,2048]{1,0:T(8,128)(2,1)S(1)}, bf16[256,2048]{1,0:T(8,128)(2,1)}, u32[]{:S(2)}) copy-start(bf16[256,2048]{1,0:T(8,128)(2,1)} %all-gather.9.cloned.1.call-done) | copy-start | bytes 3145732
  249.5 145.1 %reduce-scatter.11.cloned.1.call-start = ((), (), s32[]{:S(2)}) async-start(), calls=%async_computation.11 | async-start | bytes 1310720 | tf_op jit(solution)/shard_map/reduce_scatter | solution.py:146
  356.8 37.8 %copy-start.2 = (bf16[64,2048]{1,0:T(8,128)(2,1)S(1)}, bf16[64,2048]{1,0:T(8,128)(2,1)}, u32[]{:S(2)}) copy-start(bf16[64,2048]{1,0:T(8,128)(2,1)} %reduce-scatter.9.cloned.1.call-done) | copy-start | bytes 786436
Sparse Core Ops, SparseCore 0:
  8.9 33.5 all-gather.4
  95.8 17.6 reduce-scatter.6
  115.8 25.4 reduce-scatter.4
  143.4 15.1 all-gather.6
  165.8 27.2 reduce-scatter.8
  202.3 26.2 all-gather.8
  249.6 93.3 all-gather.10
  367.3 27.2 reduce-scatter.10
